TPU v7x, 32 devices: a whole 2x2x4 slice. The times are simulated.
32 devices in a mesh: cuts: 8 (over z, x), mode: 4 (over y, core).
Axes of the slice: x: 2, y: 2, z: 4, core: 2. Of those that a mesh axis runs over, the one named last changes fastest.
Arguments:
- sliced_state: bfloat16 [8, 16, 4, 128, 2, 128], P(None, 'cuts', None, 'mode'), may hold values from -0.75 to 0.75
- gate_blocks: bfloat16 [32, 2, 128, 128], P('cuts'), may hold values from -0.375 to 0.375
- gate_slot: int32 [32], replicated, may hold values from 0 to 31, each once
- samples: int32 [8, 4096], replicated, may hold values from 0 to 65535
Outputs:
- amplitudes: float32 [32, 128, 2, 128], P('cuts', 'mode')
- sample_probs: float32 [8, 4096], replicated
- xeb_score: float32 [8], replicated
Inputs may be any that keep to these rules, and one draw needn't show every extreme that they name: `gate_slot`: a permutation: every gate block has its own row of gate_blocks. `samples`: flat index s * 128 * 128 + p * 128 + q.
All inputs are finite; a program needn't handle non-finite values.
Results may differ from a plain program's by a relative error of at most 0.022.
Values may be sent and summed in bfloat16 or wider, within the bound.
A program may use at most 64 MiB of HBM per device.

v0:
```python
import jax
import jax.numpy as jnp
from jax import lax
from jax.sharding import PartitionSpec as P


def from_root(array, axis, root):
    mine = lax.axis_index(axis) == root
    return lax.psum(jnp.where(mine, array, jnp.zeros_like(array)), axis)


def apply_gates(tensor, blocks):
    real_part = blocks[:, 0]
    imag_part = blocks[:, 1]
    stacked = jnp.concatenate(
        [
            jnp.concatenate([real_part, imag_part], axis=2),
            jnp.concatenate([-imag_part, real_part], axis=2),
        ],
        axis=1,
    )
    layout = tensor.shape
    flattened = tensor.reshape(layout[0], -1, 2 * layout[-1])
    product = jnp.einsum("crk,ckn->crn", flattened, stacked, preferred_element_type=jnp.float32)
    return product.astype(jnp.bfloat16).reshape(layout)


def select_rows(table, wanted):
    count = table.shape[0]
    onehot = (wanted[:, None] == jnp.arange(count, dtype=jnp.int32)[None, :]).astype(table.dtype)
    picked = jnp.dot(onehot, table.reshape(count, -1), preferred_element_type=jnp.float32)
    return picked.astype(table.dtype).reshape((wanted.shape[0],) + table.shape[1:])


def on_device(sliced_state, gate_blocks, gate_slot, samples):
    circuits = sliced_state.shape[0]
    spectator = sliced_state.shape[2]
    width = sliced_state.shape[5]
    held_count = gate_blocks.shape[0]
    layer_count = gate_slot.shape[0] // (2 * circuits)
    circuit_ids = jnp.arange(circuits, dtype=jnp.int32)
    tensor = lax.all_to_all(sliced_state, "mode", split_axis=0, concat_axis=3, tiled=True)
    local_count = tensor.shape[0]
    local_ids = lax.axis_index("mode") * local_count + jnp.arange(local_count, dtype=jnp.int32)

    def fetch_one(position):
        held_block = select_rows(gate_blocks, jnp.reshape(position % held_count, (1,)))[0]
        return from_root(held_block, "cuts", position // held_count)

    def fetch_gates(layer_index, gate_kind):
        fetched = []
        for circuit in range(local_count):
            fetched.append(
                fetch_one(
                    gate_slot[(local_ids[circuit] * layer_count + layer_index) * 2 + gate_kind]
                )
            )
        return jnp.stack(fetched, axis=0)

    for layer_index in range(layer_count):
        tensor = apply_gates(tensor, fetch_gates(layer_index, 0))
        tensor = jnp.swapaxes(tensor, 3, 5)
        tensor = apply_gates(tensor, fetch_gates(layer_index, 1))
        tensor = jnp.swapaxes(tensor, 3, 5)
    summed = jnp.sum(tensor.astype(jnp.float32), axis=1)
    summed = lax.all_to_all(
        summed.astype(jnp.bfloat16), "mode", split_axis=2, concat_axis=0, tiled=True
    ).astype(summed.dtype)
    local_rows = summed.shape[2]
    summed = summed.reshape(circuits * spectator, local_rows, 2, width)
    amplitudes = lax.psum_scatter(
        summed.astype(jnp.bfloat16), "cuts", scatter_dimension=0, tiled=True
    ).astype(jnp.float32)
    row_count = amplitudes.shape[0]
    first_row = lax.axis_index("cuts") * row_count
    first_col = lax.axis_index("mode") * local_rows
    magnitude = amplitudes[:, :, 0, :] ** 2 + amplitudes[:, :, 1, :] ** 2
    row_sums = jnp.sum(magnitude, axis=(1, 2))
    owner_circuit = (first_row + jnp.arange(row_count, dtype=jnp.int32)) // spectator
    norm_part = jnp.sum(
        jnp.where(owner_circuit[None, :] == circuit_ids[:, None], row_sums[None, :], 0.0), axis=1
    )
    plane_size = width * width
    spec_index = samples // plane_size
    row_index = samples // width % width
    col_index = samples % width
    local_row = circuit_ids[:, None] * spectator + spec_index - first_row
    local_col = row_index - first_col
    is_owned = (
        (local_row >= 0) & (local_row < row_count) & (local_col >= 0) & (local_col < local_rows)
    )
    cell_index = jnp.where(is_owned, local_row * local_rows + local_col, -1)
    cell_count = row_count * local_rows
    cell_onehot = (
        cell_index[:, :, None] == jnp.arange(cell_count, dtype=jnp.int32)[None, None, :]
    ).astype(jnp.float32)
    picked_rows = jnp.einsum(
        "csr,rw->csw",
        cell_onehot,
        magnitude.reshape(cell_count, width),
        precision=lax.Precision.HIGHEST,
    )
    col_match = col_index[:, :, None] == jnp.arange(width, dtype=jnp.int32)[None, None, :]
    sample_mass = jnp.sum(jnp.where(col_match, picked_rows, 0.0), axis=2)
    dimension_scale = float(spectator * plane_size)
    norm_total = lax.psum(norm_part, ("cuts", "mode"))
    sample_probs = lax.psum(sample_mass * dimension_scale / norm_total[:, None], ("cuts", "mode"))
    xeb_score = jnp.mean(sample_probs, axis=1)
    return (amplitudes, sample_probs, xeb_score)


def solution(mesh):
    in_specs = (P(None, "cuts", None, "mode", None, None), P("cuts", None, None, None), P(), P())
    out_specs = (P("cuts", "mode", None, None), P(), P())
    return jax.shard_map(
        on_device, mesh=mesh, in_specs=in_specs, out_specs=out_specs, check_vma=False
    )
```

profile of v0, /device:TPU:0, one launch (start us, length us, event | category | flops | bytes accessed | tf_op | source)
XLA Modules:
  0.0 402.5 jit_solution(14701239896464762398)
XLA Ops:
  7.2 0.0 all-reduce.6.cloned.1.call-start
  7.2 0.6 fusion.74
  10.4 1.6 fusion.73
  32.4 1.2 copy.56
  33.6 0.3 fusion.39
  33.9 0.7 copy.39
  34.7 0.3 fusion.40
  35.0 0.7 copy.40
  35.8 0.3 fusion.41
  36.1 0.3 fusion.42
  36.4 0.3 fusion.43
  36.7 0.3 fusion.44
  37.1 0.3 fusion.45
  37.4 0.3 fusion.46
  37.7 0.6 convert_select_fusion.5
  38.3 0.6 convert_select_fusion.4
  39.0 0.6 convert_select_fusion.3
  39.6 0.6 convert_select_fusion.2
  40.2 0.6 convert_select_fusion.1
  40.8 0.6 convert_select_fusion
  41.5 0.0 all-reduce.6.cloned.1.call-update
  41.5 4.3 %all-to-all-start = ((bf16[8,2,4,32,2,128]{5,4,3,2,1,0:T(2,128)(2,1)}), bf16[8,2,4,32,2,128]{5,4,3,2,1,0:T(2,128)(2,1)S(1)}, u32[]{:S(2)}, u32[]{:S(2)}) async-start(bf16[8,2,4,32,2,128]{5,4,3,2,1,0:T(2,128)(2,1)} %param.4), calls=%async_computation | async-start | bytes 2097152 | tf_op jit(solution)/shard_map/all_to_all | solution.py:42
  45.8 72.8 %all-reduce.6.cloned.1.call-done = (bf16[1,2,128,128]{2,3,0,1:T(8,128)(2,1)}, bf16[1,2,128,128]{2,3,0,1:T(8,128)(2,1)}, bf16[1,2,128,128]{3,2,0,1:T(8,128)(2,1)}...) async-done(((bf16[1,2,128,128]{2,3,0,1:T(8,128)(2,1)}, ...) | async-done | bytes 524304 | tf_op jit(solution)/shard_map/psum | solution.py:9
  118.6 0.9 constant_dynamic-update-slice_fusion.1
  119.5 0.9 constant_dynamic-update-slice_fusion
  120.4 0.8 constant_dynamic-update-slice_fusion.3
  121.2 0.8 constant_dynamic-update-slice_fusion.5
  122.1 0.9 constant_dynamic-update-slice_fusion.2
  123.1 1.2 copy.55
  124.4 0.7 reshape.305
  125.1 0.5 fusion.2
  125.5 0.8 reshape.306
  126.3 1.1 copy.42
  127.4 0.7 reshape.307
  128.1 0.4 convolution_convert_fusion.2
  128.6 0.3 reshape.308
  128.9 1.2 copy.43
  130.1 0.7 reshape.309
  130.8 0.4 convolution_convert_fusion.1
  131.2 0.3 reshape.310
  131.5 1.2 copy.44
  132.8 0.7 reshape.311
  133.5 0.4 convolution_convert_fusion
  133.9 0.3 reshape.312
  134.2 2.4 reduce_sum.50
  136.7 0.7 copy.45
  137.4 11.4 %all_to_all.33 = bf16[2,4,128,2,128]{4,3,1,0,2:T(2,128)(2,1)S(1)} all-to-all(bf16[2,4,128,2,128]{4,3,1,0,2:T(2,128)(2,1)S(1)} %copy.45), channel_id=1, replica_groups=mesh['cuts'=8,'mode'=4] {'mode'}, dimensions={2} | all-to-all | bytes 1048576 | tf_op jit(solution)/shard_map/all_to_all | solution.py:66
  148.8 0.1 copy.46
  148.9 0.8 copy.47
  149.8 0.0 reduce-scatter.2.cloned.1.call-update
  149.8 0.0 all-reduce.4.cloned.1.call-start
  149.9 61.7 %reduce-scatter.2.cloned.1.call-done = bf16[4,32,2,128]{3,1,2,0:T(8,128)(2,1)} async-done(((bf16[32,32,2,128]{3,1,2,0:T(8,128)(2,1)}), bf16[4,32,2,128]{3,1,2,0:T(8,128)(2,1)}) %reduce-scatter.2.cloned.1.call-update) | async-done | bytes 65552 | tf_op jit(solution)/shard_map/reduce_scatter | solution.py:71
  211.5 0.8 convert_element_type.77
  212.4 0.1 fusion.71
  212.5 0.1 select_reduce_fusion.1
  212.6 0.3 add_select_fusion.4
  212.9 40.1 %psum.78 = f32[8]{0:T(128)S(1)} all-reduce(f32[8]{0:T(128)S(1)} %select_reduce_fusion.1), channel_id=1, replica_groups=mesh['cuts'=8,'mode'=4] {'cuts','mode'}, use_global_device_ids=true, to_apply=%region_13.14 | all-reduce | flops 8 | bytes 64 | tf_op jit(solution)/shard_map/psum | solution.py:106
  252.9 15.4 %select_reduce_fusion = f32[8,4096]{1,0:T(8,128)S(1)} fusion(s32[8,4096]{1,0:T(8,128)S(1)} %get-tuple-element.23, f32[128,128,1]{1,0,2:T(8,128)S(1)} %bitcast.154, s32[8,4096]{1,0:T(8,128)S(1)} %get-tuple-element.22), kind=kOutput, calls=%fused_computation | convolution fusion | flops 6459195392 | bytes 458752 | tf_op jit(solution)/shard_map/csr,rw->csw/dot_general | solution.py:97
  268.4 0.7 multiply_divide_fusion
  269.2 0.7 copy.49
  269.9 123.0 %all-reduce.4.cloned.1.call-done = f32[8,4096]{1,0:T(8,128)} async-done(((f32[8,4096]{1,0:T(8,128)}), f32[8,4096]{1,0:T(8,128)}) %all-reduce.4.cloned.1.call-update) | async-done | bytes 131088 | tf_op jit(solution)/shard_map/psum | solution.py:107
  392.8 1.1 reduce_sum.55
  393.9 0.5 broadcast_multiply_fusion
  394.4 1.6 copy.70
  (26 shorter events, 0.2 us)
Async XLA Ops:
  7.2 111.4 %all-reduce.6.cloned.1.call-start = ((), (), s32[]{:S(2)}) async-start(), calls=%async_computation.5 | async-start | bytes 1048576 | tf_op jit(solution)/shard_map/psum | solution.py:9
  41.5 81.6 %all-to-all-start = ((bf16[8,2,4,32,2,128]{5,4,3,2,1,0:T(2,128)(2,1)}), bf16[8,2,4,32,2,128]{5,4,3,2,1,0:T(2,128)(2,1)S(1)}, u32[]{:S(2)}, u32[]{:S(2)}) async-start(bf16[8,2,4,32,2,128]{5,4,3,2,1,0:T(2,128)(2,1)} %param.4), calls=%async_computation | async-start | bytes 2097152 | tf_op jit(solution)/shard_map/all_to_all | solution.py:42
  45.8 165.8 %reduce-scatter.2.cloned.1.call-start = ((), (), s32[]{:S(2)}) async-start(), calls=%async_computation.3 | async-start | bytes 589824 | tf_op jit(solution)/shard_map/reduce_scatter | solution.py:71
  118.6 4.4 %copy-start.3 = (bf16[1,2,128,128]{3,2,0,1:T(8,128)(2,1)S(1)}, bf16[1,2,128,128]{3,2,0,1:T(8,128)(2,1)}, u32[]{:S(2)}) copy-start(bf16[1,2,128,128]{3,2,0,1:T(8,128)(2,1)} %get-tuple-element.18) | copy-start | bytes 196612
  118.6 4.4 %copy-start.2 = (bf16[1,2,128,128]{3,2,0,1:T(8,128)(2,1)S(1)}, bf16[1,2,128,128]{3,2,0,1:T(8,128)(2,1)}, u32[]{:S(2)}) copy-start(bf16[1,2,128,128]{3,2,0,1:T(8,128)(2,1)} %get-tuple-element.19) | copy-start | bytes 196612
  148.9 63.7 %copy-start.1 = (s32[8,4096]{1,0:T(8,128)S(1)}, s32[8,4096]{1,0:T(8,128)}, u32[]{:S(2)}) copy-start(s32[8,4096]{1,0:T(8,128)} %param.7) | copy-start | bytes 393220
  149.8 243.0 %all-reduce.4.cloned.1.call-start = ((), (), s32[]{:S(2)}) async-start(), calls=%async_computation.4 | async-start | bytes 262144 | tf_op jit(solution)/shard_map/psum | solution.py:107
  252.9 16.2 %copy-start = (bf16[4,32,2,128]{3,1,2,0:T(8,128)(2,1)S(1)}, bf16[4,32,2,128]{3,1,2,0:T(8,128)(2,1)}, u32[]{:S(2)}) copy-start(bf16[4,32,2,128]{3,1,2,0:T(8,128)(2,1)} %reduce-scatter.2.cloned.1.call-done) | copy-start | bytes 196612
Sparse Core Ops, SparseCore 0:
  41.6 76.9 all-reduce.5
  149.9 61.5 reduce-scatter.1
  269.3 123.5 all-reduce.3
where the time goes:
time: 403 us; the launch traced here: 402 us
  waiting for transfers between devices  257 us (64%)
  blocking collectives  51.4 us (13%)
  between operations  37.4 us (9%)
  local copies, waits for them, and re-layouts  22.5 us (6%)
  matrix products  19.5 us (5%)
  other arithmetic  9.91 us (2%)
  starting transfers between devices  4.36 us (1%)
    psum x1, waiting for transfers between devices, on_device(): lax.psum(sample_mass * dimension_scale / norm_total[:, None], ('cuts', 'm...  123 us
    psum x1, waiting for transfers between devices, from_root(): return lax.psum(jnp.where(mine, array, jnp.zeros_like(array)), axis)  72.8 us
    reduce_scatter x1, waiting for transfers between devices, on_device(): lax.psum_scatter(summed.astype(jnp.bfloat16), 'cuts', scatter_dimension=0...  61.7 us
    psum x1, blocking collectives, on_device(): norm_total = lax.psum(norm_part, ('cuts', 'mode'))  40.1 us
    dot_general x1, matrix products, on_device(): jnp.einsum('csr,rw->csw', cell_onehot, magnitude.reshape(cell_count, widt...  15.4 us
    all_to_all x1, blocking collectives, on_device(): lax.all_to_all(summed.astype(jnp.bfloat16), 'mode', split_axis=2, concat_...  11.4 us
  transfers between devices with their start and end apart: 4, of which 3 were waited for; matrix products, arithmetic and copies ran while one was open for 1% of the time, Pallas kernels for 0%

commit v1 on v0

--- a/solution.py
+++ b/solution.py
@@ -104,7 +104,10 @@
     sample_mass = jnp.sum(jnp.where(col_match, picked_rows, 0.0), axis=2)
     dimension_scale = float(spectator * plane_size)
     norm_total = lax.psum(norm_part, ("cuts", "mode"))
-    sample_probs = lax.psum(sample_mass * dimension_scale / norm_total[:, None], ("cuts", "mode"))
+    sample_probs = jnp.sum(
+        lax.all_gather(sample_mass * dimension_scale / norm_total[:, None], ("cuts", "mode")),
+        axis=0,
+    )
     xeb_score = jnp.mean(sample_probs, axis=1)
     return (amplitudes, sample_probs, xeb_score)
 

time: 403 us -> 344 us (0.85)
  waiting for transfers between devices: 257 us -> 195 us
    psum x1 -> x0, waiting for transfers between devices: 123 us -> none  [on_device(): lax.psum(sample_mass * dimension_scale / norm_total[:, None], ('cuts', 'm...]
    all_gather x0 -> x1, waiting for transfers between devices: none -> 60.1 us  [on_device(): lax.all_gather(sample_mass * dimension_scale / norm_total[:, None], ('cut...]
  transfers between devices with their start and end apart: 4 -> 4, of which waited for: 3 -> 3; matrix products, arithmetic and copies ran while one was open for 1% -> 2% of each run, Pallas kernels for 0% -> 0%
where the time goes in v1:
time: 344 us; the launch traced here: 343 us
  waiting for transfers between devices  195 us (57%)
  blocking collectives  51.7 us (15%)
  between operations  37.3 us (11%)
  local copies, waits for them, and re-layouts  22.6 us (7%)
  matrix products  19.5 us (6%)
  other arithmetic  12.8 us (4%)
  starting transfers between devices  4.36 us (1%)
    psum x1, waiting for transfers between devices, from_root(): return lax.psum(jnp.where(mine, array, jnp.zeros_like(array)), axis)  72.8 us
    reduce_scatter x1, waiting for transfers between devices, on_device(): lax.psum_scatter(summed.astype(jnp.bfloat16), 'cuts', scatter_dimension=0...  61.6 us
    all_gather x1, waiting for transfers between devices, on_device(): lax.all_gather(sample_mass * dimension_scale / norm_total[:, None], ('cut...  60.1 us
    psum x1, blocking collectives, on_device(): norm_total = lax.psum(norm_part, ('cuts', 'mode'))  40.3 us
    dot_general x1, matrix products, on_device(): jnp.einsum('csr,rw->csw', cell_onehot, magnitude.reshape(cell_count, widt...  15.4 us
    all_to_all x1, blocking collectives, on_device(): lax.all_to_all(summed.astype(jnp.bfloat16), 'mode', split_axis=2, concat_...  11.4 us
  transfers between devices with their start and end apart: 4, of which 3 were waited for; matrix products, arithmetic and copies ran while one was open for 2% of the time, Pallas kernels for 0%

profile of v1, /device:TPU:0, one launch (start us, length us, event | category | flops | bytes accessed | tf_op | source)
XLA Modules:
  0.0 342.7 jit_solution(13683426155146345401)
XLA Ops:
  7.2 0.0 all-reduce.3.cloned.1.call-start
  7.2 0.6 fusion.75
  10.4 1.6 fusion.74
  32.4 1.2 copy.56
  33.6 0.3 fusion.46
  33.9 0.3 fusion.45
  34.3 0.3 fusion.44
  34.6 0.3 fusion.43
  34.9 0.3 fusion.42
  35.2 0.3 fusion.41
  35.6 0.3 fusion.40
  35.9 0.7 copy.40
  36.6 0.3 fusion.39
  36.9 0.7 copy.39
  37.7 0.6 convert_select_fusion
  38.3 0.6 convert_select_fusion.1
  38.9 0.6 convert_select_fusion.2
  39.6 0.6 convert_select_fusion.3
  40.2 0.6 convert_select_fusion.4
  40.8 0.6 convert_select_fusion.5
  41.4 0.0 all-reduce.3.cloned.1.call-update
  41.5 4.3 %all-to-all-start = ((bf16[8,2,4,32,2,128]{5,4,3,2,1,0:T(2,128)(2,1)}), bf16[8,2,4,32,2,128]{5,4,3,2,1,0:T(2,128)(2,1)S(1)}, u32[]{:S(2)}, u32[]{:S(2)}) async-start(bf16[8,2,4,32,2,128]{5,4,3,2,1,0:T(2,128)(2,1)} %param.4), calls=%async_computation | async-start | bytes 2097152 | tf_op jit(solution)/shard_map/all_to_all | solution.py:42
  45.7 72.8 %all-reduce.3.cloned.1.call-done = (bf16[1,2,128,128]{2,3,0,1:T(8,128)(2,1)}, bf16[1,2,128,128]{2,3,0,1:T(8,128)(2,1)}, bf16[1,2,128,128]{3,2,0,1:T(8,128)(2,1)}...) async-done(((bf16[1,2,128,128]{2,3,0,1:T(8,128)(2,1)}, ...) | async-done | bytes 524304 | tf_op jit(solution)/shard_map/psum | solution.py:9
  118.6 0.8 constant_dynamic-update-slice_fusion.3
  119.4 0.8 constant_dynamic-update-slice_fusion.5
  120.3 0.9 constant_dynamic-update-slice_fusion.2
  121.2 0.8 constant_dynamic-update-slice_fusion.1
  122.0 0.9 constant_dynamic-update-slice_fusion
  122.9 0.8 constant_dynamic-update-slice_fusion.7
  123.8 0.9 constant_dynamic-update-slice_fusion.6
  124.7 1.2 copy.55
  125.9 0.7 reshape.334
  126.7 0.5 fusion.2
  127.1 0.8 reshape.335
  127.9 1.1 copy.42
  129.0 0.7 reshape.336
  129.7 0.4 convolution_convert_fusion.2
  130.1 0.3 reshape.337
  130.4 1.2 copy.43
  131.7 0.7 reshape.338
  132.4 0.4 convolution_convert_fusion.1
  132.8 0.3 reshape.339
  133.1 1.2 copy.44
  134.4 0.7 reshape.340
  135.1 0.4 convolution_convert_fusion
  135.5 0.3 reshape.341
  135.8 2.4 reduce_sum.59
  138.3 0.7 copy.45
  139.0 11.4 %all_to_all.33 = bf16[2,4,128,2,128]{4,3,1,0,2:T(2,128)(2,1)S(1)} all-to-all(bf16[2,4,128,2,128]{4,3,1,0,2:T(2,128)(2,1)S(1)} %copy.45), channel_id=1, replica_groups=mesh['cuts'=8,'mode'=4] {'mode'}, dimensions={2} | all-to-all | bytes 1048576 | tf_op jit(solution)/shard_map/all_to_all | solution.py:66
  150.4 0.1 copy.46
  150.5 0.8 copy.47
  151.4 0.0 all-gather.2.cloned.1.call-start
  151.5 61.6 %reduce-scatter.2.cloned.1.call-done = bf16[4,32,2,128]{3,1,2,0:T(8,128)(2,1)} async-done(((bf16[32,32,2,128]{3,1,2,0:T(8,128)(2,1)}), bf16[4,32,2,128]{3,1,2,0:T(8,128)(2,1)}) %reduce-scatter.2.cloned.1.call-update) | async-done | bytes 65552 | tf_op jit(solution)/shard_map/reduce_scatter | solution.py:71
  213.1 0.8 convert_element_type.77
  213.9 0.1 fusion.72
  214.0 0.1 select_reduce_fusion.1
  214.1 0.3 add_select_fusion.4
  214.4 40.3 %psum.71 = f32[8]{0:T(128)S(1)} all-reduce(f32[8]{0:T(128)S(1)} %select_reduce_fusion.1), channel_id=1, replica_groups=mesh['cuts'=8,'mode'=4] {'cuts','mode'}, use_global_device_ids=true, to_apply=%region_13.14 | all-reduce | flops 8 | bytes 64 | tf_op jit(solution)/shard_map/psum | solution.py:106
  254.7 15.4 %select_reduce_fusion = f32[8,4096]{1,0:T(8,128)S(1)} fusion(s32[8,4096]{1,0:T(8,128)S(1)} %get-tuple-element.25, f32[128,128,1]{1,0,2:T(8,128)S(1)} %bitcast.156, s32[8,4096]{1,0:T(8,128)S(1)} %get-tuple-element.24), kind=kOutput, calls=%fused_computation | convolution fusion | flops 6459195392 | bytes 458752 | tf_op jit(solution)/shard_map/csr,rw->csw/dot_general | solution.py:97
  270.2 0.7 bitcast_divide_fusion
  271.0 0.7 copy.49
  271.7 60.1 %all-gather.2.cloned.1.call-done = f32[32,8,4096]{2,1,0:T(8,128)} async-done(((f32[1,8,4096]{2,1,0:T(8,128)}), f32[32,8,4096]{2,1,0:T(8,128)}) %all-gather.2.cloned.1.call-update) | async-done | bytes 4194320 | tf_op jit(solution)/shard_map/all_gather | solution.py:108
  331.7 4.0 %fusion.71 = (f32[8]{0:T(128)S(1)}, f32[8,4096]{1,0:T(8,128)}) fusion(f32[32,8,4096]{2,1,0:T(8,128)} %all-gather.2.cloned.1.call-done), kind=kLoop, calls=%fused_computation.137 | loop fusion | flops 2064376 | bytes 4325408 | tf_op jit(solution)/shard_map/reduce_sum | solution.py:111
  335.7 0.5 broadcast_multiply_fusion
  (21 shorter events, 0.2 us)
Async XLA Ops:
  7.2 111.4 %all-reduce.3.cloned.1.call-start = ((), (), s32[]{:S(2)}) async-start(), calls=%async_computation.5 | async-start | bytes 1048576 | tf_op jit(solution)/shard_map/psum | solution.py:9
  41.5 83.2 %all-to-all-start = ((bf16[8,2,4,32,2,128]{5,4,3,2,1,0:T(2,128)(2,1)}), bf16[8,2,4,32,2,128]{5,4,3,2,1,0:T(2,128)(2,1)S(1)}, u32[]{:S(2)}, u32[]{:S(2)}) async-start(bf16[8,2,4,32,2,128]{5,4,3,2,1,0:T(2,128)(2,1)} %param.4), calls=%async_computation | async-start | bytes 2097152 | tf_op jit(solution)/shard_map/all_to_all | solution.py:42
  45.7 167.3 %reduce-scatter.2.cloned.1.call-start = ((), (), s32[]{:S(2)}) async-start(), calls=%async_computation.3 | async-start | bytes 589824 | tf_op jit(solution)/shard_map/reduce_scatter | solution.py:71
  135.5 78.6 %copy-start.1 = (s32[8,4096]{1,0:T(8,128)S(1)}, s32[8,4096]{1,0:T(8,128)}, u32[]{:S(2)}) copy-start(s32[8,4096]{1,0:T(8,128)} %param.7) | copy-start | bytes 393220
  151.4 180.3 %all-gather.2.cloned.1.call-start = ((), (), s32[]{:S(2)}) async-start(), calls=%async_computation.4 | async-start | bytes 4325376 | tf_op jit(solution)/shard_map/all_gather | solution.py:108
  254.7 16.2 %copy-start = (bf16[4,32,2,128]{3,1,2,0:T(8,128)(2,1)S(1)}, bf16[4,32,2,128]{3,1,2,0:T(8,128)(2,1)}, u32[]{:S(2)}) copy-start(bf16[4,32,2,128]{3,1,2,0:T(8,128)(2,1)} %reduce-scatter.2.cloned.1.call-done) | copy-start | bytes 196612
Sparse Core Ops, SparseCore 0:
  41.6 76.9 all-reduce.2
  151.5 61.5 reduce-scatter.1
  271.1 60.6 all-gather.1
